TPU v7x, 32 devices: a whole 2x2x4 slice. The times are simulated.
32 devices in a mesh: dp: 8 (over z, x), mp: 4 (over y, core).
Axes of the slice: x: 2, y: 2, z: 4, core: 2. Of those that a mesh axis runs over, the one named last changes fastest.
Arguments:
- acts: bfloat16 [6144, 4, 1984], P('dp', 'mp'), may hold values from -6 to 6
- grads: bfloat16 [6144, 4, 1984], P('dp', 'mp'), may hold values from -0.21875 to 0.21875
- error: bfloat16 [8, 4, 1984, 1984], P('dp', 'mp'), may hold values from -4 to 4
- momentum: float32 [4, 1984, 1984], P('mp', 'dp'), may hold values from -4 to 4
- q_start: float32 [4, 1984, 128], P('mp'), may hold values from -0.125 to 0.125
Outputs:
- error_next: bfloat16 [8, 4, 1984, 1984], P('dp', 'mp')
- momentum_next: float32 [4, 1984, 1984], P('mp', 'dp')
- q_next: float32 [4, 1984, 128], P('mp')
All inputs are finite; a program needn't handle non-finite values.
Results may differ from a plain program's by a relative error of at most 0.001.
Values sent between devices are 32-bit elements; how exact they have to be, the bound alone decides.
No kernel may reach another device: no remote copies, remote signals or barrier semaphores. Data moves between devices by JAX's collectives and lax.ppermute only.
A program may use at most 128 MiB of HBM per device.

v0:
```python
import jax
import jax.numpy as jnp
from jax import lax
from jax.sharding import PartitionSpec as P

D = 3968
PRECISE = lax.Precision.HIGHEST


def per_device(acts, grads, error, momentum, q_start):
    inputs = acts[:, 0, :]
    upstream = grads[:, 0, :]
    local_grad = lax.dot_general(
        inputs, upstream, (((0,), (0,)), ((), ())), preferred_element_type=jnp.float32
    )
    merged = local_grad + error[0, 0].astype(jnp.float32)
    warm_start = q_start[0]
    replicas = lax.axis_size("dp")
    owned_rows = momentum.shape[1]
    left_local = jnp.dot(merged, warm_start, precision=PRECISE)
    left_full = lax.psum(left_local, "dp")
    gram_matrix = jnp.dot(left_full.T, left_full, precision=PRECISE)
    cholesky_low = jnp.linalg.cholesky(gram_matrix)
    ortho_basis = lax.linalg.triangular_solve(
        cholesky_low, left_full, left_side=False, lower=True, transpose_a=True
    )
    basis_owned = lax.dynamic_slice_in_dim(
        ortho_basis, lax.axis_index("dp") * owned_rows, owned_rows, 0
    )
    right_local = lax.dot_general(merged, ortho_basis, (((0,), (0,)), ((), ())), precision=PRECISE)
    q_tile = lax.psum(right_local, "dp") / replicas
    norm_total = lax.psum(jnp.sum(q_tile * q_tile), "mp")
    rms_value = jnp.sqrt(norm_total / (D * D))
    decoded = jnp.dot(ortho_basis, q_tile.T, precision=PRECISE)
    error_next = (merged - decoded).astype(jnp.bfloat16)
    update = jnp.dot(basis_owned, q_tile.T, precision=PRECISE)
    momentum_next = 0.9 * momentum[0] + 0.1 * update / (rms_value + 1e-06)
    return (error_next[None, None], momentum_next[None], q_tile[None])


def solution(mesh):
    in_specs = (
        P("dp", "mp", None),
        P("dp", "mp", None),
        P("dp", "mp", None, None),
        P("mp", "dp", None),
        P("mp", None, None),
    )
    out_specs = (P("dp", "mp", None, None), P("mp", "dp", None), P("mp", None, None))
    return jax.shard_map(
        per_device, mesh=mesh, in_specs=in_specs, out_specs=out_specs, check_vma=False
    )
```

profile of v0, /device:TPU:0, one launch (start us, length us, event | category | flops | bytes accessed | tf_op | source)
XLA Modules:
  0.0 297.2 jit_solution(10708653032430564272)
XLA Ops:
  7.2 0.0 copy-start
  7.2 0.0 all-reduce.3.cloned.1.call-start
  7.2 1.8 copy-done
  9.0 9.3 %convert_add_fusion = f32[1984,1984]{1,0:T(8,128)S(1)} fusion(bf16[1,1,1984,1984]{3,2,1,0:T(8,128)(2,1)} %param.7, bf16[768,1,1984]{0,2,1:T(8,128)(2,1)S(1)} %copy-done, bf16[768,1,1984]{0,2,1:T(8,128)(2,1)} %param.5), kind=kOutput, calls=%fused_computation | convolution fusion | flops 6053961728 | bytes 29712384 | tf_op jit(solution)/shard_map/dot_general | solution.py:13
  18.4 5.6 %copy-done.1 = f32[1984,1984]{1,0:T(8,128)} copy-done((f32[1984,1984]{1,0:T(8,128)}, f32[1984,1984]{1,0:T(8,128)S(1)}, u32[]{:S(2)}) %copy-start.1) | copy-done | bytes 15745048
  24.0 15.3 %fusion.6 = f32[1984,128]{1,0:T(8,128)} fusion(f32[1984,1984]{1,0:T(8,128)S(1)} %convert_add_fusion, f32[1,1984,128]{2,1,0:T(8,128)} %param.9), kind=kOutput, calls=%fused_computation.9 | convolution fusion | flops 6046089216 | bytes 17776640 | tf_op jit(solution)/shard_map/dot_general | solution.py:20
  39.3 0.0 all-reduce.3.cloned.1.call-update
  39.3 0.2 all-reduce.5.cloned.1.call-start
  39.6 80.8 %all-reduce.3.cloned.1.call-done = f32[1984,128]{1,0:T(8,128)} async-done(((f32[1984,128]{1,0:T(8,128)}), f32[1984,128]{1,0:T(8,128)}) %all-reduce.3.cloned.1.call-update) | async-done | bytes 1015824 | tf_op jit(solution)/shard_map/psum | solution.py:21
  120.3 3.3 %fusion.20 = f32[128,128]{1,0:T(8,128)S(1)} fusion(f32[1984,128]{1,0:T(8,128)} %all-reduce.3.cloned.1.call-done), kind=kOutput, calls=%fused_computation.31 | convolution fusion | flops 390070272 | bytes 1081344 | tf_op jit(solution)/shard_map/dot_general | solution.py:22
  123.7 0.1 copy.8
  123.8 11.7 %cholesky.16 = f32[128,128]{1,0:T(8,128)S(1)} custom-call(f32[128,128]{1,0:T(8,128)S(1)} %fusion.16), custom_call_target="Cholesky" | custom-call | tf_op jit(solution)/shard_map/jit(cholesky)/cholesky | solution.py:23
  135.5 0.6 compare_reduce_fusion
  136.2 0.7 fusion.13
  136.9 9.8 %custom-call.6 = f32[1,128,128]{1,2,0:T(8,128)S(1)} custom-call(f32[1,128,128]{2,1,0:T(8,128)S(1)} %fusion.13), custom_call_target="InvertDiagBlocksLowerTriangular" | custom-call | tf_op jit(solution)/shard_map/triangular_solve | solution.py:24
  146.7 2.2 fusion.14
  148.8 1.0 copy-done.2
  149.8 29.9 %fusion.21 = f32[1984,128]{1,0:T(8,128)} fusion(f32[1984,1984]{1,0:T(8,128)} %copy-done.1, f32[1984,128]{1,0:T(8,128)S(1)} %fusion.14), kind=kOutput, calls=%fused_computation.32 | convolution fusion | flops 6046089216 | bytes 17776640 | tf_op jit(solution)/shard_map/dot_general | solution.py:30
  179.7 0.0 all-reduce.5.cloned.1.call-update
  179.7 77.0 %all-reduce.5.cloned.1.call-done = f32[1984,128]{1,0:T(8,128)} async-done(((f32[1984,128]{1,0:T(8,128)}), f32[1984,128]{1,0:T(8,128)}) %all-reduce.5.cloned.1.call-update) | async-done | bytes 1015824 | tf_op jit(solution)/shard_map/psum | solution.py:31
  256.8 3.0 multiply_bitcast_fusion
  259.7 6.5 %psum.23 = f32[]{:T(128)} all-reduce(f32[]{:T(128)} %get-tuple-element.4), channel_id=1, replica_groups=mesh['dp'=8,'mp'=4] {'mp'}, use_global_device_ids=true, to_apply=%region_5.6 | all-reduce | flops 1 | bytes 8 | tf_op jit(solution)/shard_map/psum | solution.py:32
  267.0 19.2 %fusion = bf16[1,1,1984,1984]{3,2,1,0:T(8,128)(2,1)} fusion(f32[1984,1984]{1,0:T(8,128)} %copy-done.1, f32[1984,128]{1,0:T(8,128)} %copy-done.2, f32[1984,128]{1,0:T(8,128)} %all-reduce.5.cloned.1.call-done), kind=kOutput, calls=%fused_computation.2 | convolution fusion | flops 6054215680 | bytes 25649152 | tf_op jit(solution)/shard_map/dot_general | solution.py:34
  286.1 4.2 %fusion.5 = f32[1,248,1984]{2,1,0:T(8,128)} fusion(f32[1,248,1984]{2,1,0:T(8,128)S(1)} %copy-done.4, f32[]{:T(128)S(6)} %add.32, f32[1984,128]{1,0:T(8,128)S(1)} %copy-done.3, f32[1984,128]{1,0:T(8,128)} %copy-done.2, s32[]{:T(128)S(6)} %select_n.8), kind=kOutput, calls=%fused_computation.8 | convolution fusion | flops 757983232 | bytes 5079048 | tf_op jit(solution)/shard_map/dot_general | solution.py:36
  (8 shorter events, 0.1 us)
Async XLA Ops:
  7.2 1.9 copy-start
  7.2 113.1 %all-reduce.3.cloned.1.call-start = ((), (), s32[]{:S(2)}) async-start(), calls=%async_computation | async-start | bytes 2031616 | tf_op jit(solution)/shard_map/psum | solution.py:21
  18.4 5.6 %copy-start.1 = (f32[1984,1984]{1,0:T(8,128)}, f32[1984,1984]{1,0:T(8,128)S(1)}, u32[]{:S(2)}) copy-start(f32[1984,1984]{1,0:T(8,128)S(1)} %convert_add_fusion) | copy-start | bytes 47235076
  39.3 217.4 %all-reduce.5.cloned.1.call-start = ((), (), s32[]{:S(2)}) async-start(), calls=%async_computation.1 | async-start | bytes 2031616 | tf_op jit(solution)/shard_map/psum | solution.py:31
  148.8 1.0 copy-start.2
  266.9 19.2 %copy-start.3 = (f32[1984,128]{1,0:T(8,128)S(1)}, f32[1984,128]{1,0:T(8,128)}, u32[]{:S(2)}) copy-start(f32[1984,128]{1,0:T(8,128)} %all-reduce.5.cloned.1.call-done) | copy-start | bytes 3047428
  267.0 19.2 %copy-start.4 = (f32[1,248,1984]{2,1,0:T(8,128)S(1)}, f32[1,248,1984]{2,1,0:T(8,128)}, u32[]{:S(2)}) copy-start(f32[1,248,1984]{2,1,0:T(8,128)} %param.8) | copy-start | bytes 5904388
Sparse Core Ops, SparseCore 0:
  39.4 80.8 all-reduce.2
  179.8 76.8 all-reduce.4
where the time goes:
time: 298 us; the launch traced here: 297 us
  waiting for transfers between devices  158 us (53%)
  matrix products  83.4 us (28%)
  other arithmetic  25.8 us (9%)
  between operations  14.8 us (5%)
  local copies, waits for them, and re-layouts  8.49 us (3%)
  blocking collectives  6.53 us (2%)
    psum x1, waiting for transfers between devices, per_device(): left_full = lax.psum(left_local, 'dp')  80.8 us
    psum x1, waiting for transfers between devices, per_device(): q_tile = lax.psum(right_local, 'dp') / replicas  77 us
    dot_general x1, matrix products, per_device(): lax.dot_general(merged, ortho_basis, (((0,), (0,)), ((), ())), precision=...  29.9 us
    dot_general x1, matrix products, per_device(): decoded = jnp.dot(ortho_basis, q_tile.T, precision=PRECISE)  19.2 us
    dot_general x1, matrix products, per_device(): left_local = jnp.dot(merged, warm_start, precision=PRECISE)  15.3 us
    another operation x3, other arithmetic, per_device(): cholesky_low = jnp.linalg.cholesky(gram_matrix)  12.4 us
    another operation x2, other arithmetic, per_device(): lax.linalg.triangular_solve(cholesky_low, left_full, left_side=False, low...  10.5 us
    dot_general x1, matrix products, per_device(): lax.dot_general(inputs, upstream, (((0,), (0,)), ((), ())), preferred_ele...  9.34 us
  transfers between devices with their start and end apart: 2, of which 2 were waited for; matrix products, arithmetic and copies ran while one was open for 0% of the time, Pallas kernels for 0%

commit v1 on v0

--- a/solution.py
+++ b/solution.py
@@ -18,7 +18,11 @@
     replicas = lax.axis_size("dp")
     owned_rows = momentum.shape[1]
     left_local = jnp.dot(merged, warm_start, precision=PRECISE)
-    left_full = lax.psum(left_local, "dp")
+    left_full = left_local
+    for hop in (1, 2, 4):
+        left_full = left_full + lax.ppermute(
+            left_full, "dp", [(dev, dev ^ hop) for dev in range(8)]
+        )
     gram_matrix = jnp.dot(left_full.T, left_full, precision=PRECISE)
     cholesky_low = jnp.linalg.cholesky(gram_matrix)
     ortho_basis = lax.linalg.triangular_solve(

time: 298 us -> 308 us (1.034)
  waiting for transfers between devices: 158 us -> 166 us
  starting transfers between devices: 0.26 us -> 7.56 us
  local copies, waits for them, and re-layouts: 8.49 us -> 3.83 us
    ppermute x0 -> x3, waiting for transfers between devices: none -> 87.1 us  [per_device(): lax.ppermute(left_full, 'dp', [(dev, dev ^ hop) for dev in range(8)])]
    psum x1 -> x0, waiting for transfers between devices: 80.8 us -> none  [per_device(): left_full = lax.psum(left_local, 'dp')]
    ppermute x0 -> x3, starting transfers between devices: none -> 7.52 us  [per_device(): lax.ppermute(left_full, 'dp', [(dev, dev ^ hop) for dev in range(8)])]
    unnamed x10 -> x12, local copies, waits for them, and re-layouts: 8.4 us -> 3.74 us
  transfers between devices with their start and end apart: 2 -> 4, of which waited for: 2 -> 4; matrix products, arithmetic and copies ran while one was open for 0% -> 0% of each run, Pallas kernels for 0% -> 0%
where the time goes in v1:
time: 308 us; the launch traced here: 307 us
  waiting for transfers between devices  166 us (54%)
  matrix products  82.4 us (27%)
  other arithmetic  26.1 us (8%)
  between operations  14.9 us (5%)
  starting transfers between devices  7.56 us (2%)
  blocking collectives  6.53 us (2%)
  local copies, waits for them, and re-layouts  3.83 us (1%)
    ppermute x3, waiting for transfers between devices, per_device(): lax.ppermute(left_full, 'dp', [(dev, dev ^ hop) for dev in range(8)])  87.1 us
    psum x1, waiting for transfers between devices, per_device(): q_tile = lax.psum(right_local, 'dp') / replicas  79 us
    dot_general x1, matrix products, per_device(): lax.dot_general(merged, ortho_basis, (((0,), (0,)), ((), ())), precision=...  29.9 us
    dot_general x1, matrix products, per_device(): decoded = jnp.dot(ortho_basis, q_tile.T, precision=PRECISE)  19.2 us
    dot_general x1, matrix products, per_device(): left_local = jnp.dot(merged, warm_start, precision=PRECISE)  15.8 us
    another operation x3, other arithmetic, per_device(): cholesky_low = jnp.linalg.cholesky(gram_matrix)  12.4 us
    another operation x2, other arithmetic, per_device(): lax.linalg.triangular_solve(cholesky_low, left_full, left_side=False, low...  10.5 us
    dot_general x1, matrix products, per_device(): lax.dot_general(inputs, upstream, (((0,), (0,)), ((), ())), preferred_ele...  9.34 us
  transfers between devices with their start and end apart: 4, of which 4 were waited for; matrix products, arithmetic and copies ran while one was open for 0% of the time, Pallas kernels for 0%

profile of v1, /device:TPU:0, one launch (start us, length us, event | category | flops | bytes accessed | tf_op | source)
XLA Modules:
  0.0 307.5 jit_solution(16255628074430396967)
XLA Ops:
  7.2 1.8 copy-done
  9.0 9.3 %convert_add_fusion = f32[1984,1984]{1,0:T(8,128)S(1)} fusion(bf16[1,1,1984,1984]{3,2,1,0:T(8,128)(2,1)} %param.7, bf16[768,1,1984]{0,2,1:T(8,128)(2,1)S(1)} %copy-done, bf16[768,1,1984]{0,2,1:T(8,128)(2,1)} %param.5), kind=kOutput, calls=%fused_computation | convolution fusion | flops 6053961728 | bytes 29712384 | tf_op jit(solution)/shard_map/dot_general | solution.py:13
  18.4 15.8 %fusion.6 = f32[1984,128]{1,0:T(8,128)S(1)} fusion(f32[1984,1984]{1,0:T(8,128)S(1)} %convert_add_fusion, f32[1,1984,128]{2,1,0:T(8,128)} %param.9), kind=kOutput, calls=%fused_computation.9 | convolution fusion | flops 6046089216 | bytes 17776640 | tf_op jit(solution)/shard_map/dot_general | solution.py:20
  34.2 3.0 collective-permute-start
  37.2 22.5 %collective-permute-done = f32[1984,128]{1,0:T(8,128)S(1)} collective-permute-done((f32[1984,128]{1,0:T(8,128)S(1)}, f32[1984,128]{1,0:T(8,128)S(1)}, u32[]{:S(2)}, u32[]{:S(2)}) %collective-permute-start) | collective-permute-done | bytes 1015840 | tf_op jit(solution)/shard_map/ppermute | solution.py:23
  59.7 0.1 add.37
  59.8 1.9 collective-permute-start.1
  61.7 21.8 %collective-permute-done.1 = f32[1984,128]{1,0:T(8,128)S(1)} collective-permute-done((f32[1984,128]{1,0:T(8,128)S(1)}, f32[1984,128]{1,0:T(8,128)S(1)}, u32[]{:S(2)}, u32[]{:S(2)}) %collective-permute-start.1) | collective-permute-done | bytes 1015840 | tf_op jit(solution)/shard_map/ppermute | solution.py:23
  83.6 2.6 collective-permute-start.2
  86.2 42.9 %collective-permute-done.2 = f32[1984,128]{1,0:T(8,128)S(1)} collective-permute-done((f32[1984,128]{1,0:T(8,128)S(1)}, f32[1984,128]{1,0:T(8,128)S(1)}, u32[]{:S(2)}, u32[]{:S(2)}) %collective-permute-start.2) | collective-permute-done | bytes 1015840 | tf_op jit(solution)/shard_map/ppermute | solution.py:23
  129.2 0.9 copy-done.2
  130.1 1.8 fusion.20
  132.1 11.7 %cholesky.16 = f32[128,128]{1,0:T(8,128)S(1)} custom-call(f32[128,128]{1,0:T(8,128)S(1)} %fusion.16), custom_call_target="Cholesky" | custom-call | tf_op jit(solution)/shard_map/jit(cholesky)/cholesky | solution.py:27
  143.8 0.6 compare_reduce_fusion
  144.5 0.7 fusion.13
  145.1 9.8 %custom-call.6 = f32[1,128,128]{1,2,0:T(8,128)S(1)} custom-call(f32[1,128,128]{2,1,0:T(8,128)S(1)} %fusion.13), custom_call_target="InvertDiagBlocksLowerTriangular" | custom-call | tf_op jit(solution)/shard_map/triangular_solve | solution.py:28
  155.0 2.2 fusion.14
  157.1 1.0 copy-done.3
  158.1 29.9 %fusion.21 = f32[1984,128]{1,0:T(8,128)} fusion(f32[1984,1984]{1,0:T(8,128)} %copy-done.1, f32[1984,128]{1,0:T(8,128)S(1)} %fusion.14), kind=kOutput, calls=%fused_computation.32 | convolution fusion | flops 6046089216 | bytes 17776640 | tf_op jit(solution)/shard_map/dot_general | solution.py:34
  188.0 79.0 %all-reduce.2.cloned.1.call-done = f32[1984,128]{1,0:T(8,128)} async-done(((f32[1984,128]{1,0:T(8,128)}), f32[1984,128]{1,0:T(8,128)}) %all-reduce.2.cloned.1.call-update) | async-done | bytes 1015824 | tf_op jit(solution)/shard_map/psum | solution.py:35
  267.0 3.0 multiply_bitcast_fusion
  270.0 6.5 %psum.15 = f32[]{:T(128)} all-reduce(f32[]{:T(128)} %get-tuple-element.4), channel_id=1, replica_groups=mesh['dp'=8,'mp'=4] {'mp'}, use_global_device_ids=true, to_apply=%region_4.5 | all-reduce | flops 1 | bytes 8 | tf_op jit(solution)/shard_map/psum | solution.py:36
  277.2 19.2 %fusion = bf16[1,1,1984,1984]{3,2,1,0:T(8,128)(2,1)} fusion(f32[1984,1984]{1,0:T(8,128)} %copy-done.1, f32[1984,128]{1,0:T(8,128)} %copy-done.3, f32[1984,128]{1,0:T(8,128)} %all-reduce.2.cloned.1.call-done), kind=kOutput, calls=%fused_computation.2 | convolution fusion | flops 6054215680 | bytes 25649152 | tf_op jit(solution)/shard_map/dot_general | solution.py:38
  296.4 4.2 %fusion.5 = f32[1,248,1984]{2,1,0:T(8,128)} fusion(f32[1,248,1984]{2,1,0:T(8,128)S(1)} %copy-done.5, f32[]{:T(128)S(6)} %add.42, f32[1984,128]{1,0:T(8,128)S(1)} %copy-done.4, f32[1984,128]{1,0:T(8,128)} %copy-done.3, s32[]{:T(128)S(6)} %select_n.8), kind=kOutput, calls=%fused_computation.8 | convolution fusion | flops 757983232 | bytes 5079048 | tf_op jit(solution)/shard_map/dot_general | solution.py:40
  (16 shorter events, 0.4 us)
Async XLA Ops:
  7.2 1.9 copy-start
  7.2 259.9 %all-reduce.2.cloned.1.call-start = ((), (), s32[]{:S(2)}) async-start(), calls=%async_computation | async-start | bytes 2031616 | tf_op jit(solution)/shard_map/psum | solution.py:35
  18.4 15.8 %copy-start.1 = (f32[1984,1984]{1,0:T(8,128)}, f32[1984,1984]{1,0:T(8,128)S(1)}, u32[]{:S(2)}) copy-start(f32[1984,1984]{1,0:T(8,128)S(1)} %convert_add_fusion) | copy-start | bytes 47235076
  34.2 25.5 %collective-permute-start = (f32[1984,128]{1,0:T(8,128)S(1)}, f32[1984,128]{1,0:T(8,128)S(1)}, u32[]{:S(2)}, u32[]{:S(2)}) collective-permute-start(f32[1984,128]{1,0:T(8,128)S(1)} %fusion.6), channel_id=1, source_target_pairs={{0,4},{4,0},{8,12},{12,8},{16,20},{20,16},{24,28},{28,24},{1,5},{5... | collective-permute-start | bytes 3047432 | tf_op jit(solution)/shard_map/ppermute | solution.py:23
  59.8 23.7 %collective-permute-start.1 = (f32[1984,128]{1,0:T(8,128)S(1)}, f32[1984,128]{1,0:T(8,128)S(1)}, u32[]{:S(2)}, u32[]{:S(2)}) collective-permute-start(f32[1984,128]{1,0:T(8,128)S(1)} %add.37), channel_id=1, source_target_pairs={{0,8},{4,12},{8,0},{12,4},{16,24},{20,28},{24,16},{28,20},{1,9},{5... | collective-permute-start | bytes 3047432 | tf_op jit(solution)/shard_map/ppermute | solution.py:23
  83.6 45.5 %collective-permute-start.2 = (f32[1984,128]{1,0:T(8,128)S(1)}, f32[1984,128]{1,0:T(8,128)S(1)}, u32[]{:S(2)}, u32[]{:S(2)}) collective-permute-start(f32[1984,128]{1,0:T(8,128)S(1)} %add.38), channel_id=1, source_target_pairs={{0,16},{4,20},{8,24},{12,28},{16,0},{20,4},{24,8},{28,12},{1,17},{... | collective-permute-start | bytes 3047432 | tf_op jit(solution)/shard_map/ppermute | solution.py:23
  129.2 1.0 copy-start.2
  157.1 1.0 copy-start.3
  277.2 19.2 %copy-start.4 = (f32[1984,128]{1,0:T(8,128)S(1)}, f32[1984,128]{1,0:T(8,128)}, u32[]{:S(2)}) copy-start(f32[1984,128]{1,0:T(8,128)} %all-reduce.2.cloned.1.call-done) | copy-start | bytes 3047428
  277.2 19.2 %copy-start.5 = (f32[1,248,1984]{2,1,0:T(8,128)S(1)}, f32[1,248,1984]{2,1,0:T(8,128)}, u32[]{:S(2)}) copy-start(f32[1,248,1984]{2,1,0:T(8,128)} %param.8) | copy-start | bytes 5904388
Sparse Core Ops, SparseCore 0:
  188.1 78.8 all-reduce.1
